TPU v7x, 32 devices: a whole 2x2x4 slice. The times are simulated.
32 devices in a mesh: ep: 4 (over z), tp: 8 (over y, x, core).
Axes of the slice: x: 2, y: 2, z: 4, core: 2. Of those that a mesh axis runs over, the one named last changes fastest.
Arguments:
- tokens: bfloat16 [384, 3072], P('ep', 'tp'), may hold values from -6 to 6
- cotangent: bfloat16 [384, 3072], P('ep', 'tp'), may hold values from -6 to 6
- expert_ids: int32 [384, 2], P('ep'), may hold values from 0 to 3, all different within a row; in each aligned block of 96 rows (0 to 95, 96 to 191, ...) at most 80 rows name the same one
- combine_weights: float32 [384, 2], P('ep'), may hold values from 0.1 to 1
- w_gate: bfloat16 [4, 3072, 8192], P('ep', None, 'tp'), may hold values from -0.15625 to 0.15625
- w_up: bfloat16 [4, 3072, 8192], P('ep', None, 'tp'), may hold values from -0.109375 to 0.109375
- w_down: bfloat16 [4, 8192, 3072], P('ep', 'tp'), may hold values from -0.09375 to 0.09375
Outputs:
- mixed: bfloat16 [384, 3072], P('ep', 'tp')
- grad_tokens: bfloat16 [384, 3072], P('ep', 'tp')
- grad_combine: float32 [384, 2], P('ep')
- grad_gate: bfloat16 [4, 3072, 8192], P('ep', 'tp')
- grad_up: bfloat16 [4, 3072, 8192], P('ep', 'tp')
- grad_down: bfloat16 [4, 8192, 3072], P('ep', None, 'tp')
Inputs may be any that keep to these rules, and one draw needn't show every extreme that they name: `expert_ids`: each row names 2 different experts. Among the 96 rows of one index of ep, no expert is named more than 80 times, and in some such blocks one expert is named exactly 80 times.
All inputs are finite; a program needn't handle non-finite values.
Results may differ from a plain program's by a relative error of at most 0.019.
Values may be sent and summed in bfloat16 or wider, within the bound.
A program may use at most 128 MiB of HBM per device.

v0:
```python
import jax
import jax.numpy as jnp
from jax import lax
from jax.sharding import PartitionSpec as P


def silu_parts(gate_pre):
    sigma = jax.nn.sigmoid(gate_pre)
    return (gate_pre * sigma, sigma * (1.0 + gate_pre * (1.0 - sigma)))


def contract_rows(left, right):
    return lax.dot_general(
        left, right, (((0,), (0,)), ((), ())), preferred_element_type=jnp.float32
    )


def contract_cols(left, right):
    return lax.dot_general(
        left, right, (((1,), (1,)), ((), ())), preferred_element_type=jnp.float32
    )


def body(tokens, cotangent, expert_ids, combine_weights, w_gate, w_up, w_down):
    groups = lax.axis_size("ep")
    tok_rows, piece_width = tokens.shape
    chosen = expert_ids.shape[1]
    capacity = tok_rows * chosen * 5 // (3 * groups)
    buffer_rows = groups * capacity
    gate_weight = w_gate[0]
    up_weight = w_up[0]
    down_weight = w_down[0]
    hidden_width = gate_weight.shape[1]
    flat_ids = expert_ids.reshape(-1)
    onehot = (flat_ids[:, None] == jnp.arange(groups, dtype=jnp.int32)[None, :]).astype(jnp.int32)
    rank = jnp.sum((jnp.cumsum(onehot, axis=0) - onehot) * onehot, axis=1)
    slot_index = flat_ids * capacity + rank
    places = (jnp.arange(buffer_rows, dtype=jnp.int32)[:, None] == slot_index[None, :]).astype(
        jnp.bfloat16
    )
    placer = jnp.sum(
        places.reshape(buffer_rows, tok_rows, chosen).astype(jnp.float32), axis=2
    ).astype(jnp.bfloat16)
    scaled = (combine_weights[:, :, None] * cotangent[:, None, :].astype(jnp.float32)).astype(
        jnp.bfloat16
    )
    send_grad = jnp.dot(
        places, scaled.reshape(tok_rows * chosen, piece_width), preferred_element_type=jnp.float32
    ).astype(jnp.bfloat16)
    send_rows = jnp.dot(placer, tokens, preferred_element_type=jnp.float32).astype(jnp.bfloat16)
    recv_rows, recv_grad = (
        lax.all_to_all(
            send_rows.reshape(groups, capacity, piece_width),
            "ep",
            split_axis=0,
            concat_axis=0,
            tiled=True,
        ),
        lax.all_to_all(
            send_grad.reshape(groups, capacity, piece_width),
            "ep",
            split_axis=0,
            concat_axis=0,
            tiled=True,
        ),
    )
    recv_rows = recv_rows.reshape(buffer_rows, piece_width)
    piece = lax.all_gather(recv_rows, "tp", axis=1, tiled=True)
    gate_pre = jnp.dot(piece, gate_weight, preferred_element_type=jnp.float32)
    up_pre = jnp.dot(piece, up_weight, preferred_element_type=jnp.float32)
    recv_grad = recv_grad.reshape(buffer_rows, piece_width)
    active, slope = silu_parts(gate_pre)
    hidden = (active * up_pre).astype(jnp.bfloat16)
    partial_value = jnp.dot(hidden, down_weight, preferred_element_type=jnp.float32)
    out_piece = lax.psum_scatter(
        partial_value.astype(jnp.bfloat16), "tp", scatter_dimension=1, tiled=True
    )
    out_back = lax.all_to_all(
        out_piece.reshape(groups, capacity, piece_width),
        "ep",
        split_axis=0,
        concat_axis=0,
        tiled=True,
    ).reshape(buffer_rows, piece_width)
    out_tokens = (
        jnp.take(out_back, slot_index, axis=0)
        .reshape(tok_rows, chosen, piece_width)
        .astype(jnp.float32)
    )
    mixed = jnp.sum(combine_weights[:, :, None] * out_tokens, axis=1).astype(jnp.bfloat16)
    local_products = jnp.sum(cotangent.astype(jnp.float32)[:, None, :] * out_tokens, axis=2)
    grad_combine = lax.psum(local_products, "tp")
    grad_hidden = contract_cols(lax.all_gather(recv_grad, "tp", axis=1, tiled=True), down_weight)
    down_grad = contract_rows(hidden, lax.all_gather(recv_grad, "tp", axis=1, tiled=True))
    grad_gate_pre = (grad_hidden * up_pre * slope).astype(jnp.bfloat16)
    grad_up_pre = (grad_hidden * active).astype(jnp.bfloat16)
    input_partial = contract_cols(grad_gate_pre, gate_weight) + contract_cols(
        grad_up_pre, up_weight
    )
    input_piece = lax.psum_scatter(
        input_partial.astype(jnp.bfloat16), "tp", scatter_dimension=1, tiled=True
    )
    input_back = lax.all_to_all(
        input_piece.reshape(groups, capacity, piece_width),
        "ep",
        split_axis=0,
        concat_axis=0,
        tiled=True,
    ).reshape(buffer_rows, piece_width)
    grad_tokens = jnp.sum(
        jnp.take(input_back, slot_index, axis=0)
        .reshape(tok_rows, chosen, piece_width)
        .astype(jnp.float32),
        axis=1,
    ).astype(jnp.bfloat16)
    stacked = jnp.concatenate([grad_gate_pre, grad_up_pre], axis=1)
    both_grads = contract_rows(lax.all_gather(recv_rows, "tp", axis=1, tiled=True), stacked)
    gate_grad = both_grads[:, :hidden_width].astype(jnp.bfloat16)
    up_grad = both_grads[:, hidden_width:].astype(jnp.bfloat16)
    gate_rows_out, up_rows_out = (
        lax.all_to_all(gate_grad, "tp", split_axis=0, concat_axis=1, tiled=True),
        lax.all_to_all(up_grad, "tp", split_axis=0, concat_axis=1, tiled=True),
    )
    down_cols_out = lax.all_to_all(
        down_grad.astype(jnp.bfloat16), "tp", split_axis=1, concat_axis=0, tiled=True
    )
    return (
        mixed,
        grad_tokens,
        grad_combine,
        gate_rows_out[None],
        up_rows_out[None],
        down_cols_out[None],
    )


def solution(mesh):
    placed = (
        P("ep", "tp"),
        P("ep", "tp"),
        P("ep", None),
        P("ep", None),
        P("ep", None, "tp"),
        P("ep", None, "tp"),
        P("ep", "tp", None),
    )
    return jax.shard_map(
        body,
        mesh=mesh,
        in_specs=placed,
        out_specs=(
            P("ep", "tp"),
            P("ep", "tp"),
            P("ep", None),
            P("ep", "tp", None),
            P("ep", "tp", None),
            P("ep", None, "tp"),
        ),
        check_vma=False,
    )
```

profile of v0, /device:TPU:0, one launch (start us, length us, event | category | flops | bytes accessed | tf_op | source)
XLA Modules:
  0.0 508.4 jit_solution(12819426446226769640)
XLA Ops:
  7.2 0.0 all-gather.5.cloned.1.call-start
  7.2 0.8 copy.55
  8.0 0.1 eq.43
  8.2 1.2 reduce-window.6
  9.4 0.1 slice.26
  9.5 0.1 copy.56
  9.7 0.1 copy.57
  9.8 0.1 add_bitcast_fusion
  9.9 1.0 mul.83
  10.8 0.2 mul.84
  11.1 0.8 copy.54
  11.8 0.1 mul.81
  12.0 0.3 convolution_convert_fusion.2
  12.3 14.8 %all_to_all.68 = bf16[4,80,384]{2,1,0:T(8,128)(2,1)} all-to-all(bf16[4,80,384]{2,1,0:T(8,128)(2,1)S(1)} %bitcast.77), channel_id=1, replica_groups=mesh['ep'=4,'tp'=8] {'ep'}, dimensions={0} | all-to-all | bytes 491520 | tf_op jit(solution)/shard_map/all_to_all | solution.py:59
  27.1 0.0 all-gather.5.cloned.1.call-update
  27.1 0.0 all-gather.3.cloned.1.call-start
  27.2 0.1 reduce_sum.56
  27.3 0.1 copy.58
  27.4 0.1 fusion.27
  27.5 0.3 convolution_convert_fusion.3
  27.8 10.8 %all_to_all.69 = bf16[4,80,384]{2,1,0:T(8,128)(2,1)} all-to-all(bf16[4,80,384]{2,1,0:T(8,128)(2,1)S(1)} %bitcast.78), channel_id=1, replica_groups=mesh['ep'=4,'tp'=8] {'ep'}, dimensions={0} | all-to-all | bytes 491520 | tf_op jit(solution)/shard_map/all_to_all | solution.py:52
  38.5 0.0 all-gather.3.cloned.1.call-update
  38.6 0.0 reduce-scatter.9.cloned.1.call-start
  38.6 15.3 %all-gather.5.cloned.1.call-done = bf16[320,3072]{1,0:T(8,128)(2,1)} async-done(((bf16[320,384]{1,0:T(8,128)(2,1)}), bf16[320,3072]{1,0:T(8,128)(2,1)}) %all-gather.5.cloned.1.call-update) | async-done | bytes 1966096 | tf_op jit(solution)/shard_map/all_gather | solution.py:93
  53.9 6.7 %fusion = f32[320,1024]{1,0:T(8,128)} fusion(bf16[320,3072]{1,0:T(8,128)(2,1)} %all-gather.5.cloned.1.call-done, bf16[1,1024,3072]{2,1,0:T(8,128)(2,1)} %param.15), kind=kOutput, calls=%fused_computation.4 | convolution fusion | flops 2013265920 | bytes 9568256 | tf_op jit(solution)/shard_map/dot_general | solution.py:19
  60.6 22.8 %all-gather.3.cloned.1.call-done = bf16[320,3072]{1,0:T(8,128)(2,1)} async-done(((bf16[320,384]{1,0:T(8,128)(2,1)}), bf16[320,3072]{1,0:T(8,128)(2,1)}) %all-gather.3.cloned.1.call-update) | async-done | bytes 1966096 | tf_op jit(solution)/shard_map/all_gather | solution.py:68
  83.3 5.7 %fusion.6 = f32[320,1024]{1,0:T(8,128)S(1)} fusion(bf16[320,3072]{1,0:T(8,128)(2,1)} %all-gather.3.cloned.1.call-done, bf16[1,3072,1024]{2,1,0:T(8,128)(2,1)} %param.14), kind=kOutput, calls=%fused_computation.10 | convolution fusion | flops 2013265920 | bytes 9568256 | tf_op jit(solution)/shard_map/dot_general | solution.py:70
  89.1 5.7 %multiply_convert_fusion.1 = (bf16[320,1024]{1,0:T(8,128)(2,1)S(1)}, bf16[320,1024]{1,0:T(8,128)(2,1)S(1)}, bf16[320,1024]{1,0:T(8,128)(2,1)S(1)}) fusion(f32[320,1024]{1,0:T(8,128)S(1)} %copy-done.6, f32[320,1024]{1,0:T(8,128)S(1)} %fusion.6, bf16[320,3072]{1,0:T(8,128)(2,1)S(1)} %copy-done.4, bf16[1,3072,1024]{2,1,0:T(8,128)(2,1)} %param.13), kind=kOutput, calls=%fused_computation.24 | convolution fusion | flops 2018181120 | bytes 12845056 | tf_op jit(solution)/shard_map/dot_general | solution.py:69
  94.9 2.2 fusion.4
  97.2 2.3 fusion.15
  99.4 2.4 copy.66
  101.9 0.2 reduce-scatter.7.cloned.1.call-start
  102.1 5.0 fusion.18
  107.1 2.4 copy.64
  109.5 34.8 %reduce-scatter.9.cloned.1.call-done = bf16[384,320]{1,0:T(8,128)(2,1)} async-done(((bf16[3072,320]{1,0:T(8,128)(2,1)}), bf16[384,320]{1,0:T(8,128)(2,1)}) %reduce-scatter.9.cloned.1.call-update) | async-done | bytes 245776
  144.4 1.8 copy.67
  146.2 4.6 all-to-all-start.3
  150.8 10.9 %convolution_convert_fusion = bf16[3072,2048]{1,0:T(8,128)(2,1)} fusion(bf16[320,3072]{1,0:T(8,128)(2,1)S(1)} %copy-done.5, bf16[320,1024]{1,0:T(8,128)(2,1)} %copy-done.8, bf16[320,1024]{1,0:T(8,128)(2,1)} %copy-done.7), kind=kOutput, calls=%fused_computation.2 | convolution fusion | flops 4035444736 | bytes 15859712 | tf_op jit(solution)/shard_map/dot_general | solution.py:13
  161.7 28.8 %reduce-scatter.7.cloned.1.call-done = bf16[384,320]{1,0:T(8,128)(2,1)} async-done(((bf16[3072,320]{1,0:T(8,128)(2,1)}), bf16[384,320]{1,0:T(8,128)(2,1)}) %reduce-scatter.7.cloned.1.call-update) | async-done | bytes 245776
  190.5 1.8 copy.65
  192.3 4.6 all-to-all-start.1
  196.9 10.4 %fusion.32 = (bf16[3072,1024]{1,0:T(8,128)(2,1)}, bf16[3072,1024]{1,0:T(8,128)(2,1)}) fusion(bf16[3072,2048]{1,0:T(8,128)(2,1)} %convolution_convert_fusion), kind=kLoop, calls=%fused_computation.55 | loop fusion | bytes 25165824 | tf_op jit(solution)/shard_map/slice | solution.py:119
  207.4 76.9 %all_to_all.70 = bf16[8,384,1024]{2,1,0:T(8,128)(2,1)} all-to-all(bf16[8,384,1024]{2,1,0:T(8,128)(2,1)} %bitcast.69), channel_id=1, replica_groups=mesh['ep'=4,'tp'=8] {'tp'}, dimensions={0} | all-to-all | bytes 12582912 | tf_op jit(solution)/shard_map/all_to_all | solution.py:121
  284.2 4.9 all-to-all-start.5
  289.1 3.7 convolution_convert_fusion.1
  292.8 3.3 copy.72
  296.1 64.6 %all-to-all-done.5 = bf16[8,384,1024]{2,1,0:T(8,128)(2,1)} async-done(((bf16[8,384,1024]{2,1,0:T(8,128)(2,1)}), bf16[8,384,1024]{2,1,0:T(8,128)(2,1)}, u32[]{:S(2)}, u32[]{:S(2)}) %all-to-all-start.5) | async-done | bytes 6291488 | tf_op jit(solution)/shard_map/all_to_all | solution.py:122
  360.7 4.8 all-to-all-start.6
  365.5 1.0 gather_fusion.1
  366.5 1.0 gather_fusion
  367.5 0.1 broadcast_select_fusion
  367.7 0.2 reshape.111
  367.8 0.1 reshape.109
  367.9 0.2 multiply_reduce_fusion
  368.1 0.1 reduce_sum.61
  368.2 85.9 %psum.7 = f32[96,2]{1,0:T(8,128)S(1)} all-reduce(f32[96,2]{1,0:T(8,128)S(1)} %reduce_sum.61), channel_id=1, replica_groups=mesh['ep'=4,'tp'=8] {'tp'}, use_global_device_ids=true, to_apply=%region_9.11 | all-reduce | flops 192 | bytes 1536 | tf_op jit(solution)/shard_map/psum | solution.py:92
  454.2 0.6 copy.63
  454.8 1.0 reduce_sum.59
  455.8 1.1 multiply_reduce_fusion.1
  456.9 9.0 %copy.60 = bf16[384,8,1024]{2,1,0:T(8,128)(2,1)} copy(bf16[384,8,1024]{2,0,1:T(8,128)(2,1)} %bitcast.66) | data formatting | bytes 12582912 | tf_op jit(solution)/shard_map/all_to_all | solution.py:121
  465.9 10.4 %broadcast_in_dim.15 = bf16[1,384,8192]{2,1,0:T(8,128)(2,1)} reshape(bf16[384,8,1024]{2,1,0:T(8,128)(2,1)} %copy.60) | data formatting | bytes 12582912 | tf_op jit(solution)/shard_map/broadcast_in_dim | solution.py:131
  476.3 9.0 %copy.61 = bf16[384,8,1024]{2,1,0:T(8,128)(2,1)} copy(bf16[384,8,1024]{2,0,1:T(8,128)(2,1)} %bitcast.16) | data formatting | bytes 12582912 | tf_op jit(solution)/shard_map/all_to_all | solution.py:122
  485.3 10.4 %broadcast_in_dim.26 = bf16[1,384,8192]{2,1,0:T(8,128)(2,1)} reshape(bf16[384,8,1024]{2,1,0:T(8,128)(2,1)} %copy.61) | data formatting | bytes 12582912 | tf_op jit(solution)/shard_map/broadcast_in_dim | solution.py:132
  495.7 6.1 %copy.75 = bf16[1,8192,384]{2,1,0:T(8,128)(2,1)} copy(bf16[1,8192,384]{2,1,0:T(8,128)(2,1)} %bitcast.18) | data formatting | bytes 12582912
  (44 shorter events, 0.2 us)
Async XLA Ops:
  7.2 20.3 %copy-start = (bf16[96,384]{1,0:T(8,128)(2,1)S(1)}, bf16[96,384]{1,0:T(8,128)(2,1)}, u32[]{:S(2)}) copy-start(bf16[96,384]{1,0:T(8,128)(2,1)} %param.9) | copy-start | bytes 221188
  7.2 20.2 %copy-start.2 = (s32[96,2]{0,1:T(2,128)S(1)}, s32[96,2]{0,1:T(2,128)}, u32[]{:S(2)}) copy-start(s32[96,2]{0,1:T(2,128)} %param.11) | copy-start | bytes 2308
  7.2 46.7 %all-gather.5.cloned.1.call-start = ((), (), s32[]{:S(2)}) async-start(), calls=%async_computation.10 | async-start | bytes 2211840 | tf_op jit(solution)/shard_map/all_gather | solution.py:93
  27.1 56.2 %all-gather.3.cloned.1.call-start = ((), (), s32[]{:S(2)}) async-start(), calls=%async_computation.9 | async-start | bytes 2211840 | tf_op jit(solution)/shard_map/all_gather | solution.py:68
  38.6 105.8 %reduce-scatter.9.cloned.1.call-start = ((), (), s32[]{:S(2)}) async-start(), calls=%async_computation.12 | async-start | bytes 2654208
  83.3 5.7 %copy-start.4 = (bf16[320,3072]{1,0:T(8,128)(2,1)S(1)}, bf16[320,3072]{1,0:T(8,128)(2,1)}, u32[]{:S(2)}) copy-start(bf16[320,3072]{1,0:T(8,128)(2,1)} %all-gather.3.cloned.1.call-done) | copy-start | bytes 5898244
  83.3 5.7 %copy-start.6 = (f32[320,1024]{1,0:T(8,128)S(1)}, f32[320,1024]{1,0:T(8,128)}, u32[]{:S(2)}) copy-start(f32[320,1024]{1,0:T(8,128)} %fusion) | copy-start | bytes 3932164
  83.3 11.5 %slice-start = ((s8[6291456]{0:T(1024)(128)(4,1)}), s8[4194304]{0:T(1024)(128)(4,1)S(1)}, s32[]{:S(2)}) async-start(s8[6291456]{0:T(1024)(128)(4,1)} %bitcast.83), calls=%async_computation.13 | async-start | bytes 8388608
  83.3 13.8 %slice-start.2 = ((s8[6291456]{0:T(1024)(128)(4,1)}), s8[4194304]{0:T(1024)(128)(4,1)S(1)}, s32[]{:S(2)}) async-start(s8[6291456]{0:T(1024)(128)(4,1)} %bitcast.85), calls=%async_computation.15 | async-start | bytes 8388608
  89.1 5.8 %slice-start.1 = ((s8[6291456]{0:T(1024)(128)(4,1)}), s8[2097152]{0:T(1024)(128)(4,1)S(1)}, s32[]{:S(2)}) async-start(s8[6291456]{0:T(1024)(128)(4,1)} %bitcast.83), calls=%async_computation.14 | async-start | bytes 4194304
  89.1 8.1 %slice-start.3 = ((s8[6291456]{0:T(1024)(128)(4,1)}), s8[2097152]{0:T(1024)(128)(4,1)S(1)}, s32[]{:S(2)}) async-start(s8[6291456]{0:T(1024)(128)(4,1)} %bitcast.85), calls=%async_computation.16 | async-start | bytes 4194304
  94.8 2.3 copy-start.8
  94.8 2.3 copy-start.7
  101.9 88.6 %reduce-scatter.7.cloned.1.call-start = ((), (), s32[]{:S(2)}) async-start(), calls=%async_computation.11 | async-start | bytes 2654208
  109.5 41.3 %copy-start.5 = (bf16[320,3072]{1,0:T(8,128)(2,1)S(1)}, bf16[320,3072]{1,0:T(8,128)(2,1)}, u32[]{:S(2)}) copy-start(bf16[320,3072]{1,0:T(8,128)(2,1)} %all-gather.3.cloned.1.call-done) | copy-start | bytes 5898244
  146.2 46.2 %all-to-all-start.3 = ((bf16[4,80,384]{2,1,0:T(8,128)(2,1)}), bf16[4,80,384]{2,1,0:T(8,128)(2,1)S(1)}, u32[]{:S(2)}, u32[]{:S(2)}) async-start(bf16[4,80,384]{2,1,0:T(8,128)(2,1)} %bitcast.11), calls=%async_computation.3 | async-start | bytes 491520 | tf_op jit(solution)/shard_map/all_to_all | solution.py:103
  192.3 15.0 %all-to-all-start.1 = ((bf16[4,80,384]{2,1,0:T(8,128)(2,1)}), bf16[4,80,384]{2,1,0:T(8,128)(2,1)S(1)}, u32[]{:S(2)}, u32[]{:S(2)}) async-start(bf16[4,80,384]{2,1,0:T(8,128)(2,1)} %bitcast.7), calls=%async_computation.1 | async-start | bytes 491520 | tf_op jit(solution)/shard_map/all_to_all | solution.py:78
  284.2 4.9 copy-start.3
  284.2 76.5 %all-to-all-start.5 = ((bf16[8,384,1024]{2,1,0:T(8,128)(2,1)}), bf16[8,384,1024]{2,1,0:T(8,128)(2,1)}, u32[]{:S(2)}, u32[]{:S(2)}) async-start(bf16[8,384,1024]{2,1,0:T(8,128)(2,1)} %bitcast.68), calls=%async_computation.5 | async-start | bytes 12582912 | tf_op jit(solution)/shard_map/all_to_all | solution.py:122
  360.7 135.0 %all-to-all-start.6 = ((bf16[1024,8,384]{2,0,1:T(8,128)(2,1)}), bf16[1024,8,384]{2,0,1:T(8,128)(2,1)}, u32[]{:S(2)}, u32[]{:S(2)}) async-start(bf16[1024,8,384]{2,0,1:T(8,128)(2,1)} %bitcast.67), calls=%async_computation.6 | async-start | bytes 12582912 | tf_op jit(solution)/shard_map/all_to_all | solution.py:124
  495.7 6.2 %copy-start.1 = (bf16[96,384]{1,0:T(8,128)(2,1)S(1)}, bf16[96,384]{1,0:T(8,128)(2,1)}, u32[]{:S(2)}) copy-start(bf16[96,384]{1,0:T(8,128)(2,1)} %param.9) | copy-start | bytes 221188
Sparse Core Ops, SparseCore 0:
  27.2 26.6 all-gather.4
  55.8 27.5 all-gather.2
  102.0 42.3 reduce-scatter.8
  148.2 42.3 reduce-scatter.6
where the time goes:
time: 510 us; the launch traced here: 508 us
  blocking collectives  188 us (37%)
  waiting for transfers between devices  166 us (33%)
  local copies, waits for them, and re-layouts  73.7 us (14%)
  matrix products  42.8 us (8%)
  starting transfers between devices  19.2 us (4%)
  between operations  14.1 us (3%)
    psum x1, blocking collectives, body(): grad_combine = lax.psum(local_products, 'tp')  85.9 us
    all_to_all x1, blocking collectives, body(): lax.all_to_all(gate_grad, 'tp', split_axis=0, concat_axis=1, tiled=True)  76.9 us
    all_to_all x1, waiting for transfers between devices, body(): lax.all_to_all(up_grad, 'tp', split_axis=0, concat_axis=1, tiled=True)  64.6 us
    unnamed x6, waiting for transfers between devices  63.7 us
    all_gather x1, waiting for transfers between devices, body(): piece = lax.all_gather(recv_rows, 'tp', axis=1, tiled=True)  22.8 us
    unnamed x35, local copies, waits for them, and re-layouts  16.9 us
    all_gather x1, waiting for transfers between devices, body(): lax.all_gather(recv_grad, 'tp', axis=1, tiled=True)  15.3 us
    all_to_all x1, blocking collectives, body(): lax.all_to_all(send_grad.reshape(groups, capacity, piece_width), 'ep', sp...  14.8 us
  transfers between devices with their start and end apart: 8, of which 5 were waited for; matrix products, arithmetic and copies ran while one was open for 18% of the time, Pallas kernels for 0%

commit v1 on v0

--- a/solution.py
+++ b/solution.py
@@ -89,7 +89,7 @@
     )
     mixed = jnp.sum(combine_weights[:, :, None] * out_tokens, axis=1).astype(jnp.bfloat16)
     local_products = jnp.sum(cotangent.astype(jnp.float32)[:, None, :] * out_tokens, axis=2)
-    grad_combine = lax.psum(local_products, "tp")
+    grad_combine = lax.all_gather(local_products, "tp").sum(axis=0)
     grad_hidden = contract_cols(lax.all_gather(recv_grad, "tp", axis=1, tiled=True), down_weight)
     down_grad = contract_rows(hidden, lax.all_gather(recv_grad, "tp", axis=1, tiled=True))
     grad_gate_pre = (grad_hidden * up_pre * slope).astype(jnp.bfloat16)

time: 510 us -> 495 us (0.971)
  blocking collectives: 188 us -> 173 us
    psum x1 -> x0, blocking collectives: 85.9 us -> none  [body(): grad_combine = lax.psum(local_products, 'tp')]
    all_gather x0 -> x1, blocking collectives: none -> 70.7 us  [body(): grad_combine = lax.all_gather(local_products, 'tp').sum(axis=0)]
    unnamed x35 -> x34, local copies, waits for them, and re-layouts: 16.9 us -> 16.2 us
where the time goes in v1:
time: 495 us; the launch traced here: 493 us
  blocking collectives  173 us (35%)
  waiting for transfers between devices  166 us (34%)
  local copies, waits for them, and re-layouts  73.1 us (15%)
  matrix products  42.8 us (9%)
  starting transfers between devices  19.2 us (4%)
  between operations  14.1 us (3%)
    all_to_all x1, blocking collectives, body(): lax.all_to_all(gate_grad, 'tp', split_axis=0, concat_axis=1, tiled=True)  76.9 us
    all_gather x1, blocking collectives, body(): grad_combine = lax.all_gather(local_products, 'tp').sum(axis=0)  70.7 us
    all_to_all x1, waiting for transfers between devices, body(): lax.all_to_all(up_grad, 'tp', split_axis=0, concat_axis=1, tiled=True)  64.6 us
    unnamed x6, waiting for transfers between devices  63.7 us
    all_gather x1, waiting for transfers between devices, body(): piece = lax.all_gather(recv_rows, 'tp', axis=1, tiled=True)  22.8 us
    unnamed x34, local copies, waits for them, and re-layouts  16.2 us
    all_gather x1, waiting for transfers between devices, body(): lax.all_gather(recv_grad, 'tp', axis=1, tiled=True)  15.3 us
    all_to_all x1, blocking collectives, body(): lax.all_to_all(send_grad.reshape(groups, capacity, piece_width), 'ep', sp...  14.8 us
  transfers between devices with their start and end apart: 8, of which 5 were waited for; matrix products, arithmetic and copies ran while one was open for 18% of the time, Pallas kernels for 0%

profile of v1, /device:TPU:0, one launch (start us, length us, event | category | flops | bytes accessed | tf_op | source)
XLA Modules:
  0.0 493.1 jit_solution(14174219294558121443)
XLA Ops:
  7.2 0.0 all-gather.5.cloned.1.call-start
  7.2 0.8 copy.58
  8.0 0.1 eq.43
  8.2 1.2 reduce-window.6
  9.4 0.1 slice.26
  9.5 0.1 copy.59
  9.7 0.1 copy.60
  9.8 0.1 add_bitcast_fusion
  9.9 1.0 mul.83
  10.8 0.2 mul.84
  11.1 0.8 copy.57
  11.8 0.1 mul.81
  12.0 0.3 convolution_convert_fusion.2
  12.3 14.8 %all_to_all.68 = bf16[4,80,384]{2,1,0:T(8,128)(2,1)} all-to-all(bf16[4,80,384]{2,1,0:T(8,128)(2,1)S(1)} %bitcast.77), channel_id=1, replica_groups=mesh['ep'=4,'tp'=8] {'ep'}, dimensions={0} | all-to-all | bytes 491520 | tf_op jit(solution)/shard_map/all_to_all | solution.py:59
  27.1 0.0 all-gather.5.cloned.1.call-update
  27.1 0.0 all-gather.3.cloned.1.call-start
  27.2 0.1 reduce_sum.63
  27.3 0.1 copy.61
  27.4 0.1 fusion.27
  27.5 0.3 convolution_convert_fusion.3
  27.8 10.8 %all_to_all.69 = bf16[4,80,384]{2,1,0:T(8,128)(2,1)} all-to-all(bf16[4,80,384]{2,1,0:T(8,128)(2,1)S(1)} %bitcast.78), channel_id=1, replica_groups=mesh['ep'=4,'tp'=8] {'ep'}, dimensions={0} | all-to-all | bytes 491520 | tf_op jit(solution)/shard_map/all_to_all | solution.py:52
  38.6 0.0 reduce-scatter.9.cloned.1.call-start
  38.6 15.3 %all-gather.5.cloned.1.call-done = bf16[320,3072]{1,0:T(8,128)(2,1)} async-done(((bf16[320,384]{1,0:T(8,128)(2,1)}), bf16[320,3072]{1,0:T(8,128)(2,1)}) %all-gather.5.cloned.1.call-update) | async-done | bytes 1966096 | tf_op jit(solution)/shard_map/all_gather | solution.py:93
  53.9 6.7 %fusion = f32[320,1024]{1,0:T(8,128)} fusion(bf16[320,3072]{1,0:T(8,128)(2,1)} %all-gather.5.cloned.1.call-done, bf16[1,1024,3072]{2,1,0:T(8,128)(2,1)} %param.15), kind=kOutput, calls=%fused_computation.4 | convolution fusion | flops 2013265920 | bytes 9568256 | tf_op jit(solution)/shard_map/dot_general | solution.py:19
  60.6 22.8 %all-gather.3.cloned.1.call-done = bf16[320,3072]{1,0:T(8,128)(2,1)} async-done(((bf16[320,384]{1,0:T(8,128)(2,1)}), bf16[320,3072]{1,0:T(8,128)(2,1)}) %all-gather.3.cloned.1.call-update) | async-done | bytes 1966096 | tf_op jit(solution)/shard_map/all_gather | solution.py:68
  83.3 5.7 %fusion.6 = f32[320,1024]{1,0:T(8,128)S(1)} fusion(bf16[320,3072]{1,0:T(8,128)(2,1)} %all-gather.3.cloned.1.call-done, bf16[1,3072,1024]{2,1,0:T(8,128)(2,1)} %param.14), kind=kOutput, calls=%fused_computation.10 | convolution fusion | flops 2013265920 | bytes 9568256 | tf_op jit(solution)/shard_map/dot_general | solution.py:70
  89.1 5.7 %multiply_convert_fusion.1 = (bf16[320,1024]{1,0:T(8,128)(2,1)S(1)}, bf16[320,1024]{1,0:T(8,128)(2,1)S(1)}, bf16[320,1024]{1,0:T(8,128)(2,1)S(1)}) fusion(f32[320,1024]{1,0:T(8,128)S(1)} %copy-done.6, f32[320,1024]{1,0:T(8,128)S(1)} %fusion.6, bf16[320,3072]{1,0:T(8,128)(2,1)S(1)} %copy-done.4, bf16[1,3072,1024]{2,1,0:T(8,128)(2,1)} %param.13), kind=kOutput, calls=%fused_computation.24 | convolution fusion | flops 2018181120 | bytes 12845056 | tf_op jit(solution)/shard_map/dot_general | solution.py:69
  94.9 2.2 fusion.4
  97.2 2.3 fusion.15
  99.4 2.4 copy.71
  101.9 0.2 reduce-scatter.7.cloned.1.call-start
  102.1 5.0 %fusion.18 = bf16[320,3072]{1,0:T(8,128)(2,1)S(1)} fusion(bf16[320,1024]{1,0:T(8,128)(2,1)S(1)} %get-tuple-element.31, bf16[1,1024,3072]{2,1,0:T(8,128)(2,1)} %param.15), kind=kOutput, calls=%fused_computation.19 | convolution fusion | flops 2014248960 | bytes 8912896 | tf_op jit(solution)/shard_map/dot_general | solution.py:74
  107.1 2.4 copy.69
  109.5 34.8 %reduce-scatter.9.cloned.1.call-done = bf16[384,320]{1,0:T(8,128)(2,1)} async-done(((bf16[3072,320]{1,0:T(8,128)(2,1)}), bf16[384,320]{1,0:T(8,128)(2,1)}) %reduce-scatter.9.cloned.1.call-update) | async-done | bytes 245776
  144.4 1.8 copy.72
  146.2 4.6 all-to-all-start.3
  150.8 10.9 %convolution_convert_fusion = bf16[3072,2048]{1,0:T(8,128)(2,1)} fusion(bf16[320,3072]{1,0:T(8,128)(2,1)S(1)} %copy-done.5, bf16[320,1024]{1,0:T(8,128)(2,1)} %copy-done.8, bf16[320,1024]{1,0:T(8,128)(2,1)} %copy-done.7), kind=kOutput, calls=%fused_computation.2 | convolution fusion | flops 4035444736 | bytes 15859712 | tf_op jit(solution)/shard_map/dot_general | solution.py:13
  161.7 28.8 %reduce-scatter.7.cloned.1.call-done = bf16[384,320]{1,0:T(8,128)(2,1)} async-done(((bf16[3072,320]{1,0:T(8,128)(2,1)}), bf16[384,320]{1,0:T(8,128)(2,1)}) %reduce-scatter.7.cloned.1.call-update) | async-done | bytes 245776
  190.5 1.8 copy.70
  192.3 4.6 all-to-all-start.1
  196.9 10.4 %fusion.32 = (bf16[3072,1024]{1,0:T(8,128)(2,1)}, bf16[3072,1024]{1,0:T(8,128)(2,1)}) fusion(bf16[3072,2048]{1,0:T(8,128)(2,1)} %convolution_convert_fusion), kind=kLoop, calls=%fused_computation.55 | loop fusion | bytes 25165824 | tf_op jit(solution)/shard_map/slice | solution.py:119
  207.4 76.9 %all_to_all.70 = bf16[8,384,1024]{2,1,0:T(8,128)(2,1)} all-to-all(bf16[8,384,1024]{2,1,0:T(8,128)(2,1)} %bitcast.69), channel_id=1, replica_groups=mesh['ep'=4,'tp'=8] {'tp'}, dimensions={0} | all-to-all | bytes 12582912 | tf_op jit(solution)/shard_map/all_to_all | solution.py:121
  284.2 4.9 all-to-all-start.5
  289.1 3.7 convolution_convert_fusion.1
  292.8 3.3 copy.78
  296.1 64.6 %all-to-all-done.5 = bf16[8,384,1024]{2,1,0:T(8,128)(2,1)} async-done(((bf16[8,384,1024]{2,1,0:T(8,128)(2,1)}), bf16[8,384,1024]{2,1,0:T(8,128)(2,1)}, u32[]{:S(2)}, u32[]{:S(2)}) %all-to-all-start.5) | async-done | bytes 6291488 | tf_op jit(solution)/shard_map/all_to_all | solution.py:122
  360.7 4.8 all-to-all-start.6
  365.5 1.0 gather_fusion.1
  366.5 1.0 gather_fusion
  367.5 0.1 broadcast_select_fusion
  367.7 0.2 reshape.112
  367.8 0.1 reshape.110
  367.9 0.2 multiply_reduce_fusion
  368.1 0.1 all_gather.16
  368.2 0.1 copy.63
  368.3 1.0 reduce_sum.66
  369.3 70.7 %all_gather.17 = f32[8,96,2]{1,2,0:T(2,128)S(1)} all-gather(f32[1,96,2]{1,2,0:T(2,128)S(1)} %copy.63), channel_id=1, replica_groups=mesh['ep'=4,'tp'=8] {'tp'}, dimensions={0}, use_global_device_ids=true | all-gather | bytes 6912 | tf_op jit(solution)/shard_map/all_gather | solution.py:92
  440.0 0.6 reduce_sum.68
  440.6 1.1 multiply_reduce_fusion.1
  441.7 9.0 %copy.65 = bf16[384,8,1024]{2,1,0:T(8,128)(2,1)} copy(bf16[384,8,1024]{2,0,1:T(8,128)(2,1)} %bitcast.66) | data formatting | bytes 12582912 | tf_op jit(solution)/shard_map/all_to_all | solution.py:121
  450.7 10.4 %broadcast_in_dim.15 = bf16[1,384,8192]{2,1,0:T(8,128)(2,1)} reshape(bf16[384,8,1024]{2,1,0:T(8,128)(2,1)} %copy.65) | data formatting | bytes 12582912 | tf_op jit(solution)/shard_map/broadcast_in_dim | solution.py:131
  461.1 9.0 %copy.66 = bf16[384,8,1024]{2,1,0:T(8,128)(2,1)} copy(bf16[384,8,1024]{2,0,1:T(8,128)(2,1)} %bitcast.16) | data formatting | bytes 12582912 | tf_op jit(solution)/shard_map/all_to_all | solution.py:122
  470.0 10.4 %broadcast_in_dim.26 = bf16[1,384,8192]{2,1,0:T(8,128)(2,1)} reshape(bf16[384,8,1024]{2,1,0:T(8,128)(2,1)} %copy.66) | data formatting | bytes 12582912 | tf_op jit(solution)/shard_map/broadcast_in_dim | solution.py:132
  480.4 6.1 %copy.81 = bf16[1,8192,384]{2,1,0:T(8,128)(2,1)} copy(bf16[1,8192,384]{2,1,0:T(8,128)(2,1)} %bitcast.18) | data formatting | bytes 12582912
  (45 shorter events, 0.2 us)
Async XLA Ops:
  7.2 20.3 %copy-start = (bf16[96,384]{1,0:T(8,128)(2,1)S(1)}, bf16[96,384]{1,0:T(8,128)(2,1)}, u32[]{:S(2)}) copy-start(bf16[96,384]{1,0:T(8,128)(2,1)} %param.9) | copy-start | bytes 221188
  7.2 20.2 %copy-start.2 = (s32[96,2]{0,1:T(2,128)S(1)}, s32[96,2]{0,1:T(2,128)}, u32[]{:S(2)}) copy-start(s32[96,2]{0,1:T(2,128)} %param.11) | copy-start | bytes 2308
  7.2 46.7 %all-gather.5.cloned.1.call-start = ((), (), s32[]{:S(2)}) async-start(), calls=%async_computation.10 | async-start | bytes 2211840 | tf_op jit(solution)/shard_map/all_gather | solution.py:93
  27.1 56.2 %all-gather.3.cloned.1.call-start = ((), (), s32[]{:S(2)}) async-start(), calls=%async_computation.9 | async-start | bytes 2211840 | tf_op jit(solution)/shard_map/all_gather | solution.py:68
  38.6 105.8 %reduce-scatter.9.cloned.1.call-start = ((), (), s32[]{:S(2)}) async-start(), calls=%async_computation.12 | async-start | bytes 2654208
  83.3 5.7 %copy-start.4 = (bf16[320,3072]{1,0:T(8,128)(2,1)S(1)}, bf16[320,3072]{1,0:T(8,128)(2,1)}, u32[]{:S(2)}) copy-start(bf16[320,3072]{1,0:T(8,128)(2,1)} %all-gather.3.cloned.1.call-done) | copy-start | bytes 5898244
  83.3 5.7 %copy-start.6 = (f32[320,1024]{1,0:T(8,128)S(1)}, f32[320,1024]{1,0:T(8,128)}, u32[]{:S(2)}) copy-start(f32[320,1024]{1,0:T(8,128)} %fusion) | copy-start | bytes 3932164
  83.3 11.5 %slice-start = ((s8[6291456]{0:T(1024)(128)(4,1)}), s8[4194304]{0:T(1024)(128)(4,1)S(1)}, s32[]{:S(2)}) async-start(s8[6291456]{0:T(1024)(128)(4,1)} %bitcast.83), calls=%async_computation.13 | async-start | bytes 8388608
  83.3 13.8 %slice-start.2 = ((s8[6291456]{0:T(1024)(128)(4,1)}), s8[4194304]{0:T(1024)(128)(4,1)S(1)}, s32[]{:S(2)}) async-start(s8[6291456]{0:T(1024)(128)(4,1)} %bitcast.85), calls=%async_computation.15 | async-start | bytes 8388608
  89.1 5.8 %slice-start.1 = ((s8[6291456]{0:T(1024)(128)(4,1)}), s8[2097152]{0:T(1024)(128)(4,1)S(1)}, s32[]{:S(2)}) async-start(s8[6291456]{0:T(1024)(128)(4,1)} %bitcast.83), calls=%async_computation.14 | async-start | bytes 4194304
  89.1 8.1 %slice-start.3 = ((s8[6291456]{0:T(1024)(128)(4,1)}), s8[2097152]{0:T(1024)(128)(4,1)S(1)}, s32[]{:S(2)}) async-start(s8[6291456]{0:T(1024)(128)(4,1)} %bitcast.85), calls=%async_computation.16 | async-start | bytes 4194304
  94.8 2.3 copy-start.8
  94.8 2.3 copy-start.7
  101.9 88.6 %reduce-scatter.7.cloned.1.call-start = ((), (), s32[]{:S(2)}) async-start(), calls=%async_computation.11 | async-start | bytes 2654208
  109.5 41.3 %copy-start.5 = (bf16[320,3072]{1,0:T(8,128)(2,1)S(1)}, bf16[320,3072]{1,0:T(8,128)(2,1)}, u32[]{:S(2)}) copy-start(bf16[320,3072]{1,0:T(8,128)(2,1)} %all-gather.3.cloned.1.call-done) | copy-start | bytes 5898244
  146.2 46.2 %all-to-all-start.3 = ((bf16[4,80,384]{2,1,0:T(8,128)(2,1)}), bf16[4,80,384]{2,1,0:T(8,128)(2,1)S(1)}, u32[]{:S(2)}, u32[]{:S(2)}) async-start(bf16[4,80,384]{2,1,0:T(8,128)(2,1)} %bitcast.11), calls=%async_computation.3 | async-start | bytes 491520 | tf_op jit(solution)/shard_map/all_to_all | solution.py:103
  192.3 15.0 %all-to-all-start.1 = ((bf16[4,80,384]{2,1,0:T(8,128)(2,1)}), bf16[4,80,384]{2,1,0:T(8,128)(2,1)S(1)}, u32[]{:S(2)}, u32[]{:S(2)}) async-start(bf16[4,80,384]{2,1,0:T(8,128)(2,1)} %bitcast.7), calls=%async_computation.1 | async-start | bytes 491520 | tf_op jit(solution)/shard_map/all_to_all | solution.py:78
  284.2 4.9 copy-start.3
  284.2 76.5 %all-to-all-start.5 = ((bf16[8,384,1024]{2,1,0:T(8,128)(2,1)}), bf16[8,384,1024]{2,1,0:T(8,128)(2,1)}, u32[]{:S(2)}, u32[]{:S(2)}) async-start(bf16[8,384,1024]{2,1,0:T(8,128)(2,1)} %bitcast.68), calls=%async_computation.5 | async-start | bytes 12582912 | tf_op jit(solution)/shard_map/all_to_all | solution.py:122
  360.7 119.8 %all-to-all-start.6 = ((bf16[1024,8,384]{2,0,1:T(8,128)(2,1)}), bf16[1024,8,384]{2,0,1:T(8,128)(2,1)}, u32[]{:S(2)}, u32[]{:S(2)}) async-start(bf16[1024,8,384]{2,0,1:T(8,128)(2,1)} %bitcast.67), calls=%async_computation.6 | async-start | bytes 12582912 | tf_op jit(solution)/shard_map/all_to_all | solution.py:124
  480.4 6.2 %copy-start.1 = (bf16[96,384]{1,0:T(8,128)(2,1)S(1)}, bf16[96,384]{1,0:T(8,128)(2,1)}, u32[]{:S(2)}) copy-start(bf16[96,384]{1,0:T(8,128)(2,1)} %param.9) | copy-start | bytes 221188
Sparse Core Ops, SparseCore 0:
  27.2 26.6 all-gather.4
  55.8 27.5 all-gather.2
  102.0 42.3 reduce-scatter.8
  148.2 42.3 reduce-scatter.6
